TPU v7x, 256 devices: a whole 4x4x8 slice. The times are simulated.
256 devices in a mesh: pix: 256 (over z, y, x, core).
Axes of the slice: x: 4, y: 4, z: 8, core: 2. Of those that a mesh axis runs over, the one named last changes fastest.
Arguments:
- green: float32 [16384, 6144], P('pix'), may hold values from -200 to 200, as said below
- sketch: float32 [6144, 128], P('pix'), may hold values from -0.078125 to 0.078125
Outputs:
- basis: float32 [16384, 128], P('pix')
- projection: float32 [6144, 128], P('pix')
- spectrum_gram: float32 [128, 128], replicated
Inputs may be any that keep to these rules, and one draw needn't show every extreme that they name: `green`: finite real entries; each patch's column has its own scale.
All inputs are finite; a program needn't handle non-finite values.
Results may differ from a plain program's by a relative error of at most 0.000086.
Values sent between devices are 32-bit elements; how exact they have to be, the bound alone decides.
A program may use at most 64 MiB of HBM per device.

v0:
```python
import jax
import jax.numpy as jnp
from jax import lax
from jax.sharding import Mesh
from jax.sharding import PartitionSpec as P

PATCHES = 6144
PIX = ("pix_0", "pix_1", "pix_2", "pix_3")


def in_order(tiles, dim):
    tiles = jnp.moveaxis(tiles, 0, dim)
    dims = tiles.shape
    return tiles.reshape(*dims[:dim], dims[dim] * dims[dim + 1], *dims[dim + 2 :])


def stacked_from(shard, axes, sequence):
    tiles = shard[None]
    for k in sequence:
        tiles = lax.all_gather(tiles, axes[k], axis=0, tiled=True)
    carried = [lax.axis_size(axes[k]) for k in reversed(sequence)]
    tiles = tiles.reshape(*carried, *shard.shape)
    turned = sorted(range(len(sequence)), key=lambda place: sequence[len(sequence) - 1 - place])
    return tiles.transpose(*turned, *range(len(sequence), tiles.ndim)).reshape(-1, *shard.shape)


def whole_of(shard, axes, sequence, dim):
    return in_order(stacked_from(shard, axes, sequence), dim)


def rows_for(lines, size):
    spare = -len(lines) % size
    return jnp.pad(lines, [(0, spare)] + [(0, 0)] * (lines.ndim - 1))


def sent_to_all(shard, axis):
    size = lax.axis_size(axis)
    return lax.all_to_all(
        jnp.broadcast_to(shard[None], (size, *shard.shape)), axis, 0, 0, tiled=True
    )


def whole_of_2(shard, axes, dim):
    far, near = axes
    leading = sent_to_all(shard, far)
    tiles = jnp.swapaxes(sent_to_all(leading, near), 0, 1)
    return in_order(tiles.reshape(-1, *shard.shape), dim)


def in_blocks(shard, dim, size):
    before, after = (shard.shape[:dim], shard.shape[dim + 1 :])
    return jnp.moveaxis(shard.reshape(*before, size, -1, *after), dim, 0)


def summed_on_arrival(shard, axis, dim):
    tiles = in_blocks(shard, dim, lax.axis_size(axis))
    arrived = lax.all_to_all(tiles, axis, split_axis=0, concat_axis=0, tiled=True)
    return arrived.sum(axis=0)


def summed_rows(shard, axes, dim):
    far, near = axes
    own = summed_on_arrival(in_blocks(shard, dim, lax.axis_size(far)), near, dim + 1)
    return jnp.sum(lax.all_to_all(own, far, 0, 0, tiled=True), axis=0)


def total_of(shard, axes):
    lines = shard.reshape(-1)
    padded = rows_for(lines, lax.axis_size(axes[0]) * lax.axis_size(axes[1]))
    whole = whole_of_2(summed_rows(padded, axes, 0), axes, 0)
    return lax.slice_in_dim(whole, 0, len(lines)).reshape(shard.shape)


def body(green, sketch):
    highest = lax.Precision.HIGHEST
    rows_here = green.shape[0]
    devices_pix = lax.axis_size(PIX)
    total_pixels = rows_here * devices_pix
    columns = green
    sketched = jnp.dot(
        columns,
        whole_of(sketch, PIX, (1, 0, 2, 3), 0),
        precision=highest,
        preferred_element_type=jnp.float32,
    )
    local_gram = jnp.dot(
        sketched.T, sketched, precision=highest, preferred_element_type=jnp.float32
    )
    gram = total_of(local_gram, (("pix_0", "pix_1"), ("pix_2", "pix_3")))
    lower = jnp.linalg.cholesky(gram)
    orthonormal = jax.scipy.linalg.solve_triangular(lower, sketched.T, lower=True).T
    columns = green
    projection = summed_rows(
        lax.dot_general(
            columns,
            orthonormal,
            (((0,), (0,)), ((), ())),
            precision=highest,
            preferred_element_type=jnp.float32,
        ),
        (("pix_0", "pix_1"), ("pix_2", "pix_3")),
        0,
    )
    basis = jnp.sqrt(jnp.float32(total_pixels)) * orthonormal
    local_spec = jnp.dot(
        projection.T, projection, precision=highest, preferred_element_type=jnp.float32
    )
    spectrum_gram = total_of(local_spec, (("pix_0", "pix_1"), ("pix_2", "pix_3"))) / jnp.float32(
        PATCHES
    )
    return (basis, projection, spectrum_gram)


def solution(mesh):
    split = Mesh(mesh.devices.reshape(8, 4, 4, 2), ("pix_0", "pix_1", "pix_2", "pix_3"))
    in_specs = (P(PIX, None), P(PIX, None))
    out_specs = (P(PIX, None), P(PIX, None), P())
    return jax.shard_map(body, mesh=split, in_specs=in_specs, out_specs=out_specs, check_vma=False)
```

profile of v0, /device:TPU:1, one launch (start us, length us, event | category | flops | bytes accessed | tf_op | source)
XLA Modules:
  0.0 305.1 jit_solution(14893671459518702312)
XLA Ops:
  7.2 10.7 %all-gather = f32[96,128]{1,0:T(8,128)S(1)} all-gather(f32[24,128]{1,0:T(8,128)} %param.3), channel_id=2, replica_groups=mesh['pix_0'=8,'pix_1'=4,'pix_2'=4,'pix_3'=2] {'pix_1'}, dimensions={0}, use_global_device_ids=true | all-gather | bytes 61440 | tf_op jit(solution)/shard_map/all_gather | solution.py:20
  17.9 24.3 %all_gather.13 = f32[32,24,128]{2,1,0:T(8,128)} all-gather(f32[4,24,128]{2,1,0:T(8,128)S(1)} %bitcast.49), channel_id=1, replica_groups=mesh['pix_0'=8,'pix_1'=4,'pix_2'=4,'pix_3'=2] {'pix_0'}, dimensions={0}, use_global_device_ids=true | all-gather | bytes 442368 | tf_op jit(solution)/shard_map/all_gather | solution.py:20
  42.3 36.8 %all-gather.4.cloned.1.call-done = f32[128,24,128]{2,1,0:T(8,128)} async-done(((f32[32,24,128]{2,1,0:T(8,128)}), f32[128,24,128]{2,1,0:T(8,128)}) %all-gather.4.cloned.1.call-update) | async-done | bytes 1572880 | tf_op jit(solution)/shard_map/all_gather | solution.py:20
  79.1 20.2 %all-gather.6.cloned.1.call-done = f32[256,24,128]{2,1,0:T(8,128)} async-done(((f32[128,24,128]{2,1,0:T(8,128)}), f32[256,24,128]{2,1,0:T(8,128)}) %all-gather.6.cloned.1.call-update) | async-done | bytes 3145744 | tf_op jit(solution)/shard_map/all_gather | solution.py:20
  99.3 2.3 copy.26
  101.6 2.1 fusion.4
  104.2 8.9 %all_to_all.60 = f32[8,1,2048]{2,1,0:T(1,128)S(1)} all-to-all(f32[8,1,2048]{2,1,0:T(1,128)S(1)} %reshape.47), channel_id=1, replica_groups=mesh['pix_0'=8,'pix_1'=4,'pix_2'=4,'pix_3'=2] {'pix_2','pix_3'}, dimensions={0} | all-to-all | bytes 131072 | tf_op jit(solution)/shard_map/all_to_all | solution.py:57
  114.4 18.0 %all_to_all.61 = f32[32,1,64]{2,1,0:T(1,128)S(1)} all-to-all(f32[32,1,64]{2,1,0:T(1,128)S(1)} %bitcast.50), channel_id=1, replica_groups=mesh['pix_0'=8,'pix_1'=4,'pix_2'=4,'pix_3'=2] {'pix_0','pix_1'}, dimensions={0} | all-to-all | bytes 16384 | tf_op jit(solution)/shard_map/all_to_all | solution.py:64
  132.4 11.6 %all_to_all.62 = f32[32,1,64]{2,1,0:T(1,128)S(1)} all-to-all(f32[32,1,64]{2,1,0:T(1,128)S(1)} %broadcast_in_dim.17), channel_id=1, replica_groups=mesh['pix_0'=8,'pix_1'=4,'pix_2'=4,'pix_3'=2] {'pix_0','pix_1'}, dimensions={0} | all-to-all | bytes 16384 | tf_op jit(solution)/shard_map/all_to_all | solution.py:38
  144.2 10.6 %all_to_all.63 = f32[8,1,2048]{2,1,0:T(1,128)S(1)} all-to-all(f32[8,1,2048]{2,1,0:T(1,128)S(1)} %reshape.49), channel_id=1, replica_groups=mesh['pix_0'=8,'pix_1'=4,'pix_2'=4,'pix_3'=2] {'pix_2','pix_3'}, dimensions={0} | all-to-all | bytes 131072 | tf_op jit(solution)/shard_map/all_to_all | solution.py:38
  155.9 11.7 %cholesky.16 = f32[128,128]{1,0:T(8,128)S(1)} custom-call(f32[128,128]{1,0:T(8,128)S(1)} %fusion.3), custom_call_target="Cholesky" | custom-call | tf_op jit(solution)/shard_map/jit(cholesky)/cholesky | solution.py:90
  168.9 9.8 %custom-call.7 = f32[1,128,128]{1,2,0:T(8,128)S(1)} custom-call(f32[1,128,128]{2,1,0:T(8,128)S(1)} %fusion), custom_call_target="InvertDiagBlocksLowerTriangular" | custom-call | tf_op jit(solution)/shard_map/jit(_solve_triangular)/triangular_solve | solution.py:91
  178.9 4.3 %convolution_bitcast_fusion = f32[6144,128]{0,1:T(8,128)} fusion(f32[128,64]{0,1:T(8,128)S(1)} %fusion.1, f32[64,6144]{1,0:T(8,128)S(1)} %copy-done), kind=kOutput, calls=%fused_computation | convolution fusion | flops 603979776 | bytes 4751360 | tf_op jit(solution)/shard_map/dot_general | solution.py:94
  183.2 3.6 %copy.30 = f32[6144,128]{1,0:T(8,128)} copy(f32[6144,128]{0,1:T(8,128)} %convolution_bitcast_fusion) | data formatting | bytes 6291456 | tf_op jit(solution)/shard_map/dot_general | solution.py:94
  186.8 2.1 copy.31
  188.9 41.4 %all_to_all.64 = f32[8,32,24,128]{3,2,1,0:T(8,128)} all-to-all(f32[8,32,24,128]{3,2,1,0:T(8,128)S(1)} %copy.31), channel_id=1, replica_groups=mesh['pix_0'=8,'pix_1'=4,'pix_2'=4,'pix_3'=2] {'pix_2','pix_3'}, dimensions={0} | all-to-all | bytes 6291456 | tf_op jit(solution)/shard_map/all_to_all | solution.py:57
  230.3 2.1 reduce_sum.56
  232.4 16.5 %all_to_all.65 = f32[32,24,128]{2,1,0:T(8,128)S(1)} all-to-all(f32[32,24,128]{2,1,0:T(8,128)S(1)} %reduce_sum.56), channel_id=1, replica_groups=mesh['pix_0'=8,'pix_1'=4,'pix_2'=4,'pix_3'=2] {'pix_0','pix_1'}, dimensions={0} | all-to-all | bytes 786432 | tf_op jit(solution)/shard_map/all_to_all | solution.py:64
  249.5 10.0 %all_to_all.66 = f32[8,1,2048]{2,1,0:T(1,128)S(1)} all-to-all(f32[8,1,2048]{2,1,0:T(1,128)S(1)} %reshape.51), channel_id=1, replica_groups=mesh['pix_0'=8,'pix_1'=4,'pix_2'=4,'pix_3'=2] {'pix_2','pix_3'}, dimensions={0} | all-to-all | bytes 131072 | tf_op jit(solution)/shard_map/all_to_all | solution.py:57
  260.3 12.4 %all_to_all.67 = f32[32,1,64]{2,1,0:T(1,128)S(1)} all-to-all(f32[32,1,64]{2,1,0:T(1,128)S(1)} %bitcast.52), channel_id=1, replica_groups=mesh['pix_0'=8,'pix_1'=4,'pix_2'=4,'pix_3'=2] {'pix_0','pix_1'}, dimensions={0} | all-to-all | bytes 16384 | tf_op jit(solution)/shard_map/all_to_all | solution.py:64
  272.8 11.6 %all_to_all.68 = f32[32,1,64]{2,1,0:T(1,128)S(1)} all-to-all(f32[32,1,64]{2,1,0:T(1,128)S(1)} %broadcast_in_dim.37), channel_id=1, replica_groups=mesh['pix_0'=8,'pix_1'=4,'pix_2'=4,'pix_3'=2] {'pix_0','pix_1'}, dimensions={0} | all-to-all | bytes 16384 | tf_op jit(solution)/shard_map/all_to_all | solution.py:38
  284.4 0.8 reshape.53
  285.1 6.6 %all-to-all-start.9 = ((f32[8,1,2048]{2,1,0:T(1,128)}), f32[8,1,2048]{2,1,0:T(1,128)S(1)}, u32[]{:S(2)}, u32[]{:S(2)}) async-start(f32[8,1,2048]{2,1,0:T(1,128)} %reshape.53), calls=%async_computation.9 | async-start | bytes 131072 | tf_op jit(solution)/shard_map/all_to_all | solution.py:38
  292.3 4.3 %all-to-all-done.9 = f32[8,1,2048]{2,1,0:T(1,128)S(1)} async-done(((f32[8,1,2048]{2,1,0:T(1,128)}), f32[8,1,2048]{2,1,0:T(1,128)S(1)}, u32[]{:S(2)}, u32[]{:S(2)}) %all-to-all-start.9) | async-done | bytes 65568 | tf_op jit(solution)/shard_map/all_to_all | solution.py:38
  (47 shorter events, 8.5 us)
Async XLA Ops:
  7.2 94.4 %copy-start = (f32[64,6144]{1,0:T(8,128)S(1)}, f32[64,6144]{1,0:T(8,128)}, u32[]{:S(2)}) copy-start(f32[64,6144]{1,0:T(8,128)} %param.2) | copy-start | bytes 4718596
  7.2 71.9 %all-gather.4.cloned.1.call-start = ((), (), s32[]{:S(2)}) async-start(), calls=%async_computation.10 | async-start | bytes 1966080 | tf_op jit(solution)/shard_map/all_gather | solution.py:20
  42.3 57.0 %all-gather.6.cloned.1.call-start = ((), (), s32[]{:S(2)}) async-start(), calls=%async_computation.11 | async-start | bytes 4718592 | tf_op jit(solution)/shard_map/all_gather | solution.py:20
  248.9 49.3 %copy-start.1 = (f32[24,128]{1,0:T(8,128)}, f32[24,128]{1,0:T(8,128)S(1)}, u32[]{:S(2)}) copy-start(f32[24,128]{1,0:T(8,128)S(1)} %reduce_sum.57) | copy-start | bytes 36868
  285.1 11.5 %all-to-all-start.9 = ((f32[8,1,2048]{2,1,0:T(1,128)}), f32[8,1,2048]{2,1,0:T(1,128)S(1)}, u32[]{:S(2)}, u32[]{:S(2)}) async-start(f32[8,1,2048]{2,1,0:T(1,128)} %reshape.53), calls=%async_computation.9 | async-start | bytes 131072 | tf_op jit(solution)/shard_map/all_to_all | solution.py:38
Sparse Core Ops, SparseCore 0:
  42.4 36.6 all-gather.3
  80.9 18.3 all-gather.5
where the time goes:
time: 306 us; the launch traced here: 305 us
  blocking collectives  176 us (58%)
  waiting for transfers between devices  61.2 us (20%)
  other arithmetic  28.7 us (9%)
  between operations  14.3 us (5%)
  local copies, waits for them, and re-layouts  11.3 us (4%)
  matrix products  7.14 us (2%)
  starting transfers between devices  6.69 us (2%)
    all_to_all x3, blocking collectives, summed_on_arrival(): lax.all_to_all(tiles, axis, split_axis=0, concat_axis=0, tiled=True)  60.2 us
    all_gather x2, waiting for transfers between devices, stacked_from(): tiles = lax.all_gather(tiles, axes[k], axis=0, tiled=True)  56.9 us
    all_to_all x3, blocking collectives, summed_rows(): return jnp.sum(lax.all_to_all(own, far, 0, 0, tiled=True), axis=0)  46.9 us
    all_gather x2, blocking collectives, stacked_from(): tiles = lax.all_gather(tiles, axes[k], axis=0, tiled=True)  35 us
    all_to_all x3, blocking collectives, sent_to_all(): lax.all_to_all(jnp.broadcast_to(shard[None], (size, *shard.shape)), axis,...  33.8 us
    another operation x3, other arithmetic, body(): lower = jnp.linalg.cholesky(gram)  12.4 us
    another operation x2, other arithmetic, body(): jax.scipy.linalg.solve_triangular(lower, sketched.T, lower=True)  10.5 us
    all_to_all x1, starting transfers between devices, sent_to_all(): lax.all_to_all(jnp.broadcast_to(shard[None], (size, *shard.shape)), axis,...  6.61 us
  transfers between devices with their start and end apart: 3, of which 3 were waited for; matrix products, arithmetic and copies ran while one was open for 0% of the time, Pallas kernels for 0%

commit v1 on v0

--- a/solution.py
+++ b/solution.py
@@ -17,7 +17,9 @@
 def stacked_from(shard, axes, sequence):
     tiles = shard[None]
     for k in sequence:
-        tiles = lax.all_gather(tiles, axes[k], axis=0, tiled=True)
+        tiles = jnp.concatenate(
+            lax.all_to_all(jnp.stack([tiles] * lax.axis_size(axes[k])), axes[k], 0, 0), axis=0
+        )
     carried = [lax.axis_size(axes[k]) for k in reversed(sequence)]
     tiles = tiles.reshape(*carried, *shard.shape)
     turned = sorted(range(len(sequence)), key=lambda place: sequence[len(sequence) - 1 - place])

time: 306 us -> 254 us (0.83)
  waiting for transfers between devices: 61.2 us -> 4.25 us
  blocking collectives: 176 us -> 195 us
  between operations: 14.3 us -> 0.87 us
    all_to_all x0 -> x4, blocking collectives: none -> 60.1 us  [stacked_from(): lax.all_to_all(jnp.stack([tiles] * lax.axis_size(axes[k])), axes[k], 0, 0)]
    all_gather x2 -> x0, waiting for transfers between devices: 56.9 us -> none  [stacked_from(): tiles = lax.all_gather(tiles, axes[k], axis=0, tiled=True)]
    all_gather x2 -> x0, blocking collectives: 35 us -> none  [stacked_from(): tiles = lax.all_gather(tiles, axes[k], axis=0, tiled=True)]
    all_to_all x3, blocking collectives: 46.9 us -> 42.6 us  [summed_rows(): return jnp.sum(lax.all_to_all(own, far, 0, 0, tiled=True), axis=0)]
  transfers between devices with their start and end apart: 3 -> 1, of which waited for: 3 -> 1; matrix products, arithmetic and copies ran while one was open for 0% -> 0% of each run, Pallas kernels for 0% -> 0%
where the time goes in v1:
time: 254 us
  blocking collectives  195 us (77%)
  other arithmetic  28.9 us (11%)
  local copies, waits for them, and re-layouts  10.3 us (4%)
  matrix products  7.28 us (3%)
  starting transfers between devices  6.61 us (3%)
  waiting for transfers between devices  4.25 us (2%)
    all_to_all x4, blocking collectives, stacked_from(): lax.all_to_all(jnp.stack([tiles] * lax.axis_size(axes[k])), axes[k], 0, 0)  60.1 us
    all_to_all x3, blocking collectives, summed_on_arrival(): lax.all_to_all(tiles, axis, split_axis=0, concat_axis=0, tiled=True)  58.9 us
    all_to_all x3, blocking collectives, summed_rows(): return jnp.sum(lax.all_to_all(own, far, 0, 0, tiled=True), axis=0)  42.6 us
    all_to_all x3, blocking collectives, sent_to_all(): lax.all_to_all(jnp.broadcast_to(shard[None], (size, *shard.shape)), axis,...  33.8 us
    another operation x3, other arithmetic, body(): lower = jnp.linalg.cholesky(gram)  12.4 us
    another operation x2, other arithmetic, body(): jax.scipy.linalg.solve_triangular(lower, sketched.T, lower=True)  10.5 us
    all_to_all x1, starting transfers between devices, sent_to_all(): lax.all_to_all(jnp.broadcast_to(shard[None], (size, *shard.shape)), axis,...  6.61 us
  transfers between devices with their start and end apart: 1, of which 1 were waited for; matrix products, arithmetic and copies ran while one was open for 0% of the time, Pallas kernels for 0%

profile of v1, /device:TPU:1, one launch (start us, length us, event | category | flops | bytes accessed | tf_op | source)
XLA Modules:
  0.0 253.6 jit_solution(9392008067754099413)
XLA Ops:
  0.6 0.8 stack.12
  1.5 9.2 %all_to_all.80 = f32[4,1,24,128]{3,2,1,0:T(8,128)S(1)} all-to-all(f32[4,1,24,128]{3,2,1,0:T(8,128)S(1)} %stack.12), channel_id=1, replica_groups=mesh['pix_0'=8,'pix_1'=4,'pix_2'=4,'pix_3'=2] {'pix_1'}, dimensions={0} | all-to-all | bytes 98304 | tf_op jit(solution)/shard_map/all_to_all | solution.py:21
  10.7 19.6 %all_to_all.81 = f32[8,4,24,128]{3,2,1,0:T(8,128)S(1)} all-to-all(f32[8,4,24,128]{3,2,1,0:T(8,128)S(1)} %stack.13), channel_id=1, replica_groups=mesh['pix_0'=8,'pix_1'=4,'pix_2'=4,'pix_3'=2] {'pix_0'}, dimensions={0} | all-to-all | bytes 786432 | tf_op jit(solution)/shard_map/all_to_all | solution.py:21
  30.4 20.0 %all_to_all.82 = f32[4,32,24,128]{3,2,1,0:T(8,128)S(1)} all-to-all(f32[4,32,24,128]{3,2,1,0:T(8,128)S(1)} %stack.14), channel_id=1, replica_groups=mesh['pix_0'=8,'pix_1'=4,'pix_2'=4,'pix_3'=2] {'pix_2'}, dimensions={0} | all-to-all | bytes 3145728 | tf_op jit(solution)/shard_map/all_to_all | solution.py:21
  50.6 11.3 %all_to_all.83 = f32[2,128,24,128]{3,2,1,0:T(8,128)S(1)} all-to-all(f32[2,128,24,128]{3,2,1,0:T(8,128)S(1)} %pad_maximum_fusion), channel_id=1, replica_groups=mesh['pix_0'=8,'pix_1'=4,'pix_2'=4,'pix_3'=2] {'pix_3'}, dimensions={0} | all-to-all | bytes 6291456 | tf_op jit(solution)/shard_map/all_to_all | solution.py:21
  62.3 2.2 fusion.4
  65.1 7.6 %all_to_all.84 = f32[8,1,2048]{2,1,0:T(1,128)S(1)} all-to-all(f32[8,1,2048]{2,1,0:T(1,128)S(1)} %reshape.48), channel_id=1, replica_groups=mesh['pix_0'=8,'pix_1'=4,'pix_2'=4,'pix_3'=2] {'pix_2','pix_3'}, dimensions={0} | all-to-all | bytes 131072 | tf_op jit(solution)/shard_map/all_to_all | solution.py:59
  74.0 13.7 %all_to_all.85 = f32[32,1,64]{2,1,0:T(1,128)S(1)} all-to-all(f32[32,1,64]{2,1,0:T(1,128)S(1)} %bitcast.54), channel_id=1, replica_groups=mesh['pix_0'=8,'pix_1'=4,'pix_2'=4,'pix_3'=2] {'pix_0','pix_1'}, dimensions={0} | all-to-all | bytes 16384 | tf_op jit(solution)/shard_map/all_to_all | solution.py:66
  87.8 11.6 %all_to_all.86 = f32[32,1,64]{2,1,0:T(1,128)S(1)} all-to-all(f32[32,1,64]{2,1,0:T(1,128)S(1)} %broadcast_in_dim.14), channel_id=1, replica_groups=mesh['pix_0'=8,'pix_1'=4,'pix_2'=4,'pix_3'=2] {'pix_0','pix_1'}, dimensions={0} | all-to-all | bytes 16384 | tf_op jit(solution)/shard_map/all_to_all | solution.py:40
  99.5 10.6 %all_to_all.87 = f32[8,1,2048]{2,1,0:T(1,128)S(1)} all-to-all(f32[8,1,2048]{2,1,0:T(1,128)S(1)} %reshape.50), channel_id=1, replica_groups=mesh['pix_0'=8,'pix_1'=4,'pix_2'=4,'pix_3'=2] {'pix_2','pix_3'}, dimensions={0} | all-to-all | bytes 131072 | tf_op jit(solution)/shard_map/all_to_all | solution.py:40
  111.2 11.7 %cholesky.16 = f32[128,128]{1,0:T(8,128)S(1)} custom-call(f32[128,128]{1,0:T(8,128)S(1)} %fusion.3), custom_call_target="Cholesky" | custom-call | tf_op jit(solution)/shard_map/jit(cholesky)/cholesky | solution.py:92
  124.3 9.8 %custom-call.7 = f32[1,128,128]{1,2,0:T(8,128)S(1)} custom-call(f32[1,128,128]{2,1,0:T(8,128)S(1)} %fusion), custom_call_target="InvertDiagBlocksLowerTriangular" | custom-call | tf_op jit(solution)/shard_map/jit(_solve_triangular)/triangular_solve | solution.py:93
  134.3 4.3 %convolution_bitcast_fusion = f32[6144,128]{0,1:T(8,128)} fusion(f32[128,64]{0,1:T(8,128)S(1)} %fusion.1, f32[64,6144]{1,0:T(8,128)S(1)} %copy-done), kind=kOutput, calls=%fused_computation | convolution fusion | flops 603979776 | bytes 4751360 | tf_op jit(solution)/shard_map/dot_general | solution.py:96
  138.6 3.6 %copy.30 = f32[6144,128]{1,0:T(8,128)} copy(f32[6144,128]{0,1:T(8,128)} %convolution_bitcast_fusion) | data formatting | bytes 6291456 | tf_op jit(solution)/shard_map/dot_general | solution.py:96
  142.2 2.1 copy.31
  144.3 41.4 %all_to_all.88 = f32[8,32,24,128]{3,2,1,0:T(8,128)} all-to-all(f32[8,32,24,128]{3,2,1,0:T(8,128)S(1)} %copy.31), channel_id=1, replica_groups=mesh['pix_0'=8,'pix_1'=4,'pix_2'=4,'pix_3'=2] {'pix_2','pix_3'}, dimensions={0} | all-to-all | bytes 6291456 | tf_op jit(solution)/shard_map/all_to_all | solution.py:59
  185.7 2.1 reduce_sum.56
  187.8 16.5 %all_to_all.89 = f32[32,24,128]{2,1,0:T(8,128)S(1)} all-to-all(f32[32,24,128]{2,1,0:T(8,128)S(1)} %reduce_sum.56), channel_id=1, replica_groups=mesh['pix_0'=8,'pix_1'=4,'pix_2'=4,'pix_3'=2] {'pix_0','pix_1'}, dimensions={0} | all-to-all | bytes 786432 | tf_op jit(solution)/shard_map/all_to_all | solution.py:66
  204.8 10.0 %all_to_all.90 = f32[8,1,2048]{2,1,0:T(1,128)S(1)} all-to-all(f32[8,1,2048]{2,1,0:T(1,128)S(1)} %reshape.52), channel_id=1, replica_groups=mesh['pix_0'=8,'pix_1'=4,'pix_2'=4,'pix_3'=2] {'pix_2','pix_3'}, dimensions={0} | all-to-all | bytes 131072 | tf_op jit(solution)/shard_map/all_to_all | solution.py:59
  215.6 12.4 %all_to_all.91 = f32[32,1,64]{2,1,0:T(1,128)S(1)} all-to-all(f32[32,1,64]{2,1,0:T(1,128)S(1)} %bitcast.56), channel_id=1, replica_groups=mesh['pix_0'=8,'pix_1'=4,'pix_2'=4,'pix_3'=2] {'pix_0','pix_1'}, dimensions={0} | all-to-all | bytes 16384 | tf_op jit(solution)/shard_map/all_to_all | solution.py:66
  228.1 11.6 %all_to_all.92 = f32[32,1,64]{2,1,0:T(1,128)S(1)} all-to-all(f32[32,1,64]{2,1,0:T(1,128)S(1)} %broadcast_in_dim.17), channel_id=1, replica_groups=mesh['pix_0'=8,'pix_1'=4,'pix_2'=4,'pix_3'=2] {'pix_0','pix_1'}, dimensions={0} | all-to-all | bytes 16384 | tf_op jit(solution)/shard_map/all_to_all | solution.py:40
  239.7 0.8 reshape.54
  240.5 6.6 %all-to-all-start.13 = ((f32[8,1,2048]{2,1,0:T(1,128)}), f32[8,1,2048]{2,1,0:T(1,128)S(1)}, u32[]{:S(2)}, u32[]{:S(2)}) async-start(f32[8,1,2048]{2,1,0:T(1,128)} %reshape.54), calls=%async_computation.13 | async-start | bytes 131072 | tf_op jit(solution)/shard_map/all_to_all | solution.py:40
  247.7 4.3 %all-to-all-done.13 = f32[8,1,2048]{2,1,0:T(1,128)S(1)} async-done(((f32[8,1,2048]{2,1,0:T(1,128)}), f32[8,1,2048]{2,1,0:T(1,128)S(1)}, u32[]{:S(2)}, u32[]{:S(2)}) %all-to-all-start.13) | async-done | bytes 65568 | tf_op jit(solution)/shard_map/all_to_all | solution.py:40
  (47 shorter events, 9.1 us)
Async XLA Ops:
  0.6 61.7 %copy-start = (f32[64,6144]{1,0:T(8,128)S(1)}, f32[64,6144]{1,0:T(8,128)}, u32[]{:S(2)}) copy-start(f32[64,6144]{1,0:T(8,128)} %param.2) | copy-start | bytes 4718596
  204.3 49.3 %copy-start.1 = (f32[24,128]{1,0:T(8,128)}, f32[24,128]{1,0:T(8,128)S(1)}, u32[]{:S(2)}) copy-start(f32[24,128]{1,0:T(8,128)S(1)} %reduce_sum.57) | copy-start | bytes 36868
  240.5 11.5 %all-to-all-start.13 = ((f32[8,1,2048]{2,1,0:T(1,128)}), f32[8,1,2048]{2,1,0:T(1,128)S(1)}, u32[]{:S(2)}, u32[]{:S(2)}) async-start(f32[8,1,2048]{2,1,0:T(1,128)} %reshape.54), calls=%async_computation.13 | async-start | bytes 131072 | tf_op jit(solution)/shard_map/all_to_all | solution.py:40
